TPU v7x, 8 devices: a whole 2x2x1 slice. The times are simulated.
8 devices in a mesh: dp: 1 (over z), vp: 2 (over y), tp: 4 (over x, core).
Axes of the slice: x: 2, y: 2, z: 1, core: 2. Of those that a mesh axis runs over, the one named last changes fastest.
Arguments:
- hidden: bfloat16 [64, 2048], P('dp', 'tp')
- lnf_gain: float32 [2048], P('tp')
- lnf_bias: float32 [2048], P('tp')
- emb_table: bfloat16 [250880, 2048], P('vp', 'tp')
- next_tok: int32 [64], P('dp')
- eln_gain: float32 [2048], P('tp')
- eln_bias: float32 [2048], P('tp')
Outputs:
- output 1: float32 [64, 250880], P('dp', ('vp', 'tp'))
- output 2: float32 [64], P('dp')
- output 3: bfloat16 [64, 2048], P('dp', 'tp')
All inputs are finite; a program needn't handle non-finite values.
Results may differ from a plain program's by a relative error of at most 0.001.
Values sent between devices are 32-bit elements.
A program may use at most 1 GiB of HBM per device.

v0:
```python
import jax
import jax.numpy as jnp
from jax import lax
from jax.sharding import PartitionSpec as P

NORM_EPS = 1e-5


def norm_shard(rows_in, norm_gain, norm_bias, full_width):
    rows_f32 = rows_in.astype(jnp.float32)
    row_sums = jnp.stack([jnp.sum(rows_f32, axis=1), jnp.sum(rows_f32 * rows_f32, axis=1)])
    row_sums = lax.psum(row_sums, "tp")
    row_mean = row_sums[0] / full_width
    row_var = row_sums[1] / full_width - row_mean * row_mean
    scaled = (rows_f32 - row_mean[:, None]) * lax.rsqrt(row_var + NORM_EPS)[:, None]
    return (scaled * norm_gain + norm_bias).astype(jnp.bfloat16)


def global_lse(logits):
    row_top = lax.pmax(jnp.max(logits, axis=1), ("vp", "tp"))
    exp_total = lax.psum(jnp.sum(jnp.exp(logits - row_top[:, None]), axis=1), ("vp", "tp"))
    return row_top + jnp.log(exp_total)


def solution(mesh):
    tp_size = mesh.shape["tp"]

    def per_device(hidden, lnf_gain, lnf_bias, emb_table, next_tok, eln_gain, eln_bias):
        full_width = hidden.shape[1] * tp_size
        normed = norm_shard(hidden, lnf_gain, lnf_bias, full_width)
        shard_logits = lax.dot_general(normed, emb_table, (((1,), (1,)), ((), ())), preferred_element_type=jnp.float32)
        logits = lax.psum_scatter(shard_logits, "tp", scatter_dimension=1, tiled=True)
        log_sum = global_lse(logits)
        logprobs = logits - log_sum[:, None]
        block_rows = emb_table.shape[0]
        local_idx = next_tok - lax.axis_index("vp") * block_rows
        is_owned = (local_idx >= 0) & (local_idx < block_rows)
        picked = jnp.take(emb_table, jnp.clip(local_idx, 0, block_rows - 1), axis=0).astype(jnp.float32)
        picked = jnp.where(is_owned[:, None], picked, jnp.zeros_like(picked))
        tok_rows = lax.psum(picked, "vp")
        next_in = norm_shard(tok_rows, eln_gain, eln_bias, full_width)
        return logprobs, log_sum, next_in

    return jax.shard_map(
        per_device,
        mesh=mesh,
        in_specs=(P("dp", "tp"), P("tp"), P("tp"), P("vp", "tp"), P("dp"), P("tp"), P("tp")),
        out_specs=(P("dp", ("vp", "tp")), P("dp"), P("dp", "tp")),
        check_vma=False,
    )
```

profile of v0, /device:TPU:0, one launch (start us, length us, event | category | flops | bytes accessed | tf_op | source)
XLA Modules:
  0.0 381.5 jit_solution(13671971971119426699)
XLA Ops:
  7.2 0.0 all-reduce.3.cloned.1.call-start
  7.2 0.7 compare_and_fusion
  7.9 2.4 gather_fusion
  10.3 0.7 convert_select_fusion
  11.0 0.0 all-reduce.3.cloned.1.call-update
  11.1 0.0 reduce-scatter.2.cloned.1.call-start
  11.1 1.0 convert_reduce_fusion
  12.1 17.9 %all-reduce.3.cloned.1.call-done = f32[64,512]{1,0:T(8,128)} async-done(((f32[64,512]{1,0:T(8,128)}), f32[64,512]{1,0:T(8,128)}) %all-reduce.3.cloned.1.call-update) | async-done | bytes 131088 | tf_op jit(solution)/shard_map/psum | solution.py:40
  30.0 1.0 fusion.15
  31.1 6.1 %all-reduce = (f32[2,64]{1,0:T(2,128)S(1)}, f32[2,64]{1,0:T(2,128)S(1)}) all-reduce(f32[2,64]{1,0:T(2,128)S(1)} %get-tuple-element.12, f32[2,64]{1,0:T(2,128)S(1)} %get-tuple-element.13), channel_id=1, replica_groups=mesh['dp'=1,'vp'=2,'tp'=4] {'tp'}, use_global_device_ids=true, to_apply=%region_2.0 | all-reduce | flops 256 | bytes 2048 | tf_op jit(solution)/shard_map/psum | solution.py:12
  37.2 58.2 %fusion.5 = f32[64,125440]{1,0:T(8,128)} fusion(bf16[125440,512]{1,0:T(8,128)(2,1)} %param.10, bf16[64,512]{1,0:T(8,128)(2,1)} %param.7, f32[512]{0:T(512)} %param.9, f32[512]{0:T(512)} %param.8, f32[64]{0:T(128)S(1)} %fusion.14, f32[64]{0:T(128)S(1)} %multiply_bitcast_fusion.1), kind=kOutput, calls=%fused_computation.14 | convolution fusion | flops 8221032448 | bytes 160633344 | tf_op jit(solution)/shard_map/dot_general | solution.py:31
  95.4 0.0 copy-start
  95.4 0.0 reduce-scatter.2.cloned.1.call-update
  95.4 0.8 copy-done
  96.3 0.0 copy-done.1
  96.3 0.0 copy-done.2
  96.3 0.7 add_convert_fusion
  97.0 216.1 %reduce-scatter.2.cloned.1.call-done = f32[64,31360]{1,0:T(8,128)} async-done(((f32[64,125440]{1,0:T(8,128)}), f32[64,31360]{1,0:T(8,128)}) %reduce-scatter.2.cloned.1.call-update) | async-done | bytes 8028176 | tf_op jit(solution)/shard_map/reduce_scatter | solution.py:32
  313.1 3.7 reduce_max.9
  316.8 22.2 %pmax.7 = f32[64]{0:T(128)S(1)} all-reduce(f32[64]{0:T(128)S(1)} %reduce_max.9), channel_id=1, replica_groups=mesh['dp'=1,'vp'=2,'tp'=4] {'vp','tp'}, use_global_device_ids=true, to_apply=%region_5.0 | all-reduce | flops 64 | bytes 512 | tf_op jit(solution)/shard_map/pmax | solution.py:20
  339.1 4.5 %exponential_reduce_fusion = f32[64]{0:T(128)S(1)} fusion(f32[64,31360]{1,0:T(8,128)} %reduce-scatter.2.cloned.1.call-done, f32[64]{0:T(128)S(1)} %pmax.7), kind=kLoop, calls=%fused_computation.1 | loop fusion | flops 4014016 | bytes 8028672 | tf_op jit(solution)/shard_map/reduce_sum | solution.py:21
  343.5 24.0 %psum.29 = f32[64]{0:T(128)S(1)} all-reduce(f32[64]{0:T(128)S(1)} %exponential_reduce_fusion), channel_id=1, replica_groups=mesh['dp'=1,'vp'=2,'tp'=4] {'vp','tp'}, use_global_device_ids=true, to_apply=%region_7.0 | all-reduce | flops 64 | bytes 512 | tf_op jit(solution)/shard_map/psum | solution.py:21
  367.5 7.1 %broadcast_subtract_fusion = f32[64,31360]{1,0:T(8,128)} fusion(f32[64,31360]{1,0:T(8,128)} %reduce-scatter.2.cloned.1.call-done, f32[64]{0:T(128)S(1)} %log_add_fusion), kind=kLoop, calls=%fused_computation.2 | loop fusion | flops 2007040 | bytes 16056576 | tf_op jit(solution)/shard_map/sub | solution.py:34
  374.7 0.0 copy-done.3
  (10 shorter events, 0.1 us)
Async XLA Ops:
  7.2 22.9 %all-reduce.3.cloned.1.call-start = ((), (), s32[]{:S(2)}) async-start(), calls=%async_computation.2 | async-start | bytes 262144 | tf_op jit(solution)/shard_map/psum | solution.py:40
  11.1 302.0 %reduce-scatter.2.cloned.1.call-start = ((), (), s32[]{:S(2)}) async-start(), calls=%async_computation.1 | async-start | bytes 40140800 | tf_op jit(solution)/shard_map/reduce_scatter | solution.py:32
  95.4 0.9 copy-start
  95.4 0.9 copy-start.1
  95.4 0.9 copy-start.2
  367.5 7.1 %copy-start.3 = (f32[64]{0:T(128)}, f32[64]{0:T(128)S(1)}, u32[]{:S(2)}) copy-start(f32[64]{0:T(128)S(1)} %log_add_fusion) | copy-start | bytes 772
Sparse Core Ops, SparseCore 0:
  11.2 18.7 all-reduce.2
  95.5 217.5 reduce-scatter.1
where the time goes:
time: 382 us
  waiting for transfers between devices  234 us (61%)
  matrix products  58.2 us (15%)
  blocking collectives  52.3 us (14%)
  other arithmetic  19.5 us (5%)
  between operations  14.1 us (4%)
    reduce_scatter x1, waiting for transfers between devices, per_device(): lax.psum_scatter(shard_logits, 'tp', scatter_dimension=1, tiled=True)  216 us
    dot_general x1, matrix products, per_device(): lax.dot_general(normed, emb_table, (((1,), (1,)), ((), ())), preferred_el...  58.2 us
    psum x1, blocking collectives, global_lse(): lax.psum(jnp.sum(jnp.exp(logits - row_top[:, None]), axis=1), ('vp', 'tp'))  24 us
    pmax x1, blocking collectives, global_lse(): row_top = lax.pmax(jnp.max(logits, axis=1), ('vp', 'tp'))  22.2 us
    psum x1, waiting for transfers between devices, per_device(): tok_rows = lax.psum(picked, 'vp')  17.9 us
  transfers between devices with their start and end apart: 2, of which 2 were waited for; matrix products, arithmetic and copies ran while one was open for 0% of the time, Pallas kernels for 0%

commit v1 on v0

v1 whole, which is shorter than its diff:
```python
import functools

import jax
import jax.numpy as jnp
from jax import lax
from jax.experimental import pallas as pl
from jax.experimental.pallas import tpu as pltpu
from jax.sharding import PartitionSpec as P

NORM_EPS = 1e-5
MESH = pl.DeviceIdType.MESH
F32 = jnp.float32
BF16 = jnp.bfloat16
LANES = 128


def cols_to_rows(cols):
    rows = cols[0].shape[0]
    lane = lax.broadcasted_iota(jnp.int32, (rows, LANES), 1)
    tile = jnp.zeros((rows, LANES), F32)
    for k, col in enumerate(cols):
        tile = jnp.where(lane == k, col, tile)
    full = jnp.concatenate([tile, jnp.zeros((LANES - rows, LANES), F32)], axis=0)
    return full.T[0:8, :]


def rows_to_cols(tile, rows):
    full = jnp.concatenate([tile, jnp.zeros((LANES - 8, LANES), F32)], axis=0)
    return full.T[0:rows, :]


def row_sums_tile(rows_f32):
    return cols_to_rows([
        jnp.sum(rows_f32, axis=1, keepdims=True),
        jnp.sum(rows_f32 * rows_f32, axis=1, keepdims=True),
    ])


def norm_rows(rows_f32, totals, gain, bias, full_width):
    mean = totals[0:1, :] / full_width
    var = totals[1:2, :] / full_width - mean * mean
    rstd = lax.rsqrt(var + NORM_EPS)
    pick = lax.broadcasted_iota(jnp.int32, (8, LANES), 0)
    both = jnp.where(pick == 0, mean, rstd)
    cols = rows_to_cols(both, rows_f32.shape[0])
    scaled = (rows_f32 - cols[:, 0:1]) * cols[:, 1:2]
    return (scaled * gain + bias).astype(BF16)


def logits_kernel(
    cfg, hid, gain, bias, tok, egain, ebias, tab,
    z, lse, nin,
    xn, out, xrecv, drecv, stg, tbuf, pick, ypick, runmax, runsum,
    ln_send, ln_recv, eln_send, eln_recv, fin_send, fin_recv,
    tab_sem, dsend_sem, drecv_sem, xsend_sem, xrecv_sem, ysend_sem, yrecv_sem,
    lns_sem, lnr_sem, els_sem, elr_sem, fis_sem, fir_sem,
):
    n, T, B, S, S2, n0, full_width = cfg
    rows = hid.shape[0]
    dp = lax.axis_index("dp")
    v = lax.axis_index("vp")
    t = lax.axis_index("tp")
    x = lax.div(t, 2)
    c = lax.rem(t, 2)

    def peer(d):
        pv = 1 - v if d >= 4 else v
        px = 1 - x if (d // 2) % 2 else x
        pc = 1 - c if d % 2 else c
        return (dp, pv, 2 * px + pc)

    def start_table(j):
        a = lax.div(j, n)
        i = j - a * n
        xx = (1 - x) + a * (2 * x - 1)
        for w in range(2):
            cc = 1 - c if w == 0 else c
            row = pl.multiple_of((2 * xx + cc) * B + i * T, LANES)
            slot = lax.rem(j, S)
            pltpu.make_async_copy(tab.at[pl.ds(row, T)], tbuf.at[slot, w], tab_sem.at[slot, w]).start()

    def wait_table(j, w):
        slot = lax.rem(j, S)
        pltpu.make_async_copy(tab.at[pl.ds(0, T)], tbuf.at[slot, w], tab_sem.at[slot, w]).wait()

    def first_row(j, w):
        a = lax.div(j, n)
        i = j - a * n
        xx = (1 - x) + a * (2 * x - 1)
        cc = 1 - c if w == 0 else c
        return v * (4 * B) + (2 * xx + cc) * B + i * T

    def d2d_copy(j):
        slot = lax.rem(j, S2)
        return pltpu.make_async_remote_copy(
            src_ref=stg.at[slot], dst_ref=drecv.at[j],
            send_sem=dsend_sem.at[slot], recv_sem=drecv_sem.at[j],
            device_id=peer(1), device_id_type=MESH)

    def x_copy(i):
        return pltpu.make_async_remote_copy(
            src_ref=out.at[i], dst_ref=xrecv.at[i],
            send_sem=xsend_sem.at[i], recv_sem=xrecv_sem.at[i],
            device_id=peer(2), device_id_type=MESH)

    def small_copy(src, dst, ssem, rsem, d):
        return pltpu.make_async_remote_copy(
            src_ref=src, dst_ref=dst.at[d], send_sem=ssem.at[d], recv_sem=rsem.at[d],
            device_id=peer(d), device_id_type=MESH)

    for j in range(S):
        start_table(j)

    barrier = pltpu.get_barrier_semaphore()
    for d in range(1, 8):
        pl.semaphore_signal(barrier, inc=1, device_id=peer(d), device_id_type=MESH)

    hid_f32 = hid[...].astype(F32)
    ln_send[...] = row_sums_tile(hid_f32)
    tok_cols = rows_to_cols(
        jnp.concatenate([tok[...].astype(F32), jnp.zeros((7, LANES), F32)], axis=0), rows)
    tok_col = tok_cols[:, 0:1].astype(jnp.int32)
    pick[...] = jnp.zeros_like(pick)
    runmax[...] = jnp.full(runmax.shape, -jnp.inf, F32)
    runsum[...] = jnp.zeros_like(runsum)
    pl.semaphore_wait(barrier, 7)

    for d in range(1, 4):
        small_copy(ln_send, ln_recv, lns_sem, lnr_sem, d).start()
    totals = ln_send[...]
    for d in range(1, 4):
        small_copy(ln_send, ln_recv, lns_sem, lnr_sem, d).wait()
        totals = totals + ln_recv[d]
    xn[...] = norm_rows(hid_f32, totals, gain[...], bias[...], full_width)

    def matmul(j, w):
        slot = lax.rem(j, S)
        return lax.dot_general(
            xn[...], tbuf[slot, w], (((1,), (1,)), ((), ())), preferred_element_type=F32)

    def pick_rows(j):
        slot = lax.rem(j, S)
        total = pick[...]
        for w in range(2):
            local = tok_col - first_row(j, w)
            hot = (lax.broadcasted_iota(jnp.int32, (rows, T), 1) == local).astype(F32).astype(BF16)
            total = total + jnp.dot(hot, tbuf[slot, w], preferred_element_type=F32)
        pick[...] = total

    def zcols(i):
        return pl.ds(pl.multiple_of(i * T, LANES), T)

    def send_half(j):
        wait_table(j, 0)

        @pl.when(j >= S2)
        def _():
            d2d_copy(j - S2).wait_send()

        stg[lax.rem(j, S2)] = matmul(j, 0)

    def combine_out(i):
        d2d_copy(i).wait_recv()
        out[i] = out[i] + drecv[i]

    def refill(j):
        @pl.when(j + S < 2 * n)
        def _():
            start_table(j + S)

    @pl.loop(0, n)
    def _(j):
        send_half(j)

        @pl.when(j >= 1)
        def _():
            combine_out(j - 1)

        d2d_copy(j).start()
        wait_table(j, 1)
        out[j] = matmul(j, 1)

        @pl.when(jnp.logical_and(j >= 1, j <= n0))
        def _():
            x_copy(j - 1).start()

        pick_rows(j)
        refill(j)

    @pl.loop(n, 2 * n)
    def _(j):
        send_half(j)

        @pl.when(j == n)
        def _():
            combine_out(n - 1)

        @pl.when(j > n)
        def _():
            d2d_copy(j - 1).wait_recv()
            z[:, zcols(j - 1 - n)] = z[:, zcols(j - 1 - n)] + drecv[j - 1]

        d2d_copy(j).start()
        wait_table(j, 1)
        z[:, zcols(j - n)] = matmul(j, 1)
        pick_rows(j)
        refill(j)

    d2d_copy(2 * n - 1).wait_recv()
    z[:, zcols(n - 1)] = z[:, zcols(n - 1)] + drecv[2 * n - 1]

    ycopy = pltpu.make_async_remote_copy(
        src_ref=pick, dst_ref=ypick, send_sem=ysend_sem, recv_sem=yrecv_sem,
        device_id=peer(4), device_id_type=MESH)
    ycopy.start()
    ycopy.wait()
    tok_rows = pick[...] + ypick[...]
    eln_send[...] = row_sums_tile(tok_rows)
    for d in range(1, 4):
        small_copy(eln_send, eln_recv, els_sem, elr_sem, d).start()
    for i in range(n0, n):
        x_copy(i).start()

    @pl.loop(0, n)
    def _(i):
        x_copy(i).wait_recv()
        m_old = runmax[...]
        m_new = m_old
        for k in range(T // LANES):
            cols = pl.ds(pl.multiple_of(i * T, LANES) + k * LANES, LANES)
            val = z[:, cols] + xrecv[i, :, k * LANES:(k + 1) * LANES]
            z[:, cols] = val
            m_new = jnp.maximum(m_new, val)
        s_new = runsum[...] * jnp.exp(m_old - m_new)
        for k in range(T // LANES):
            cols = pl.ds(pl.multiple_of(i * T, LANES) + k * LANES, LANES)
            s_new = s_new + jnp.exp(z[:, cols] - m_new)
        runmax[...] = m_new
        runsum[...] = s_new

    top = jnp.max(runmax[...], axis=1, keepdims=True)
    exp_sum = jnp.sum(runsum[...] * jnp.exp(runmax[...] - top), axis=1, keepdims=True)
    fin_send[...] = cols_to_rows([top, exp_sum])
    for d in range(1, 8):
        small_copy(fin_send, fin_recv, fis_sem, fir_sem, d).start()

    totals = eln_send[...]
    for d in range(1, 4):
        small_copy(eln_send, eln_recv, els_sem, elr_sem, d).wait()
        totals = totals + eln_recv[d]
    nin[...] = norm_rows(pick[...] + ypick[...], totals, egain[...], ebias[...], full_width)

    @pl.loop(0, n)
    def _(i):
        x_copy(i).wait_send()

    @pl.loop(2 * n - S2, 2 * n)
    def _(j):
        d2d_copy(j).wait_send()

    tiles = [fin_send[...]]
    for d in range(1, 8):
        small_copy(fin_send, fin_recv, fis_sem, fir_sem, d).wait()
        tiles.append(fin_recv[d])
    best = tiles[0][0:1, :]
    for tile in tiles[1:]:
        best = jnp.maximum(best, tile[0:1, :])
    total = jnp.zeros_like(best)
    for tile in tiles:
        total = total + tile[1:2, :] * jnp.exp(tile[0:1, :] - best)
    lse[...] = jnp.broadcast_to(best + jnp.log(total), lse.shape)


def finish_kernel(z, lse, nin, logp, log_sum, next_in, buf, sem):
    rows = z.shape[0]
    col = rows_to_cols(lse[...], rows)[:, 0:1]
    steps = rows // 8

    def put(b):
        return pltpu.make_async_copy(
            buf.at[pl.ds(8 * b, 8)], logp.at[pl.ds(8 * b, 8)], sem.at[b])

    for b in range(steps):
        buf[8 * b:8 * b + 8, :] = z[8 * b:8 * b + 8, :] - col[8 * b:8 * b + 8, :]
        if b >= 1:
            put(b - 1).start()
    next_in[...] = nin[...]
    log_sum[...] = lse[0:1, 0:rows]
    put(steps - 1).start()
    for b in range(steps):
        put(b).wait()


def solution(mesh):
    tp_size = mesh.shape["tp"]

    def per_device(hidden, lnf_gain, lnf_bias, emb_table, next_tok, eln_gain, eln_bias):
        rows, width = hidden.shape
        block = emb_table.shape[0] // tp_size
        T = 7 * LANES
        n = block // T
        S, S2, n0 = 3, 4, 25
        cfg = (n, T, block, S, S2, n0, float(width * tp_size))
        vmem = pl.BlockSpec(memory_space=pltpu.VMEM)
        hbm = pl.BlockSpec(memory_space=pl.ANY)
        tok_row = jnp.pad(next_tok.reshape(1, rows), ((0, 0), (0, LANES - rows)))
        dma = pltpu.SemaphoreType.DMA
        z, lse, nin = pl.pallas_call(
            functools.partial(logits_kernel, cfg),
            out_shape=(
                pltpu.VMEM((rows, block), F32),
                jax.ShapeDtypeStruct((8, LANES), F32),
                jax.ShapeDtypeStruct((rows, width), BF16),
            ),
            in_specs=[vmem] * 6 + [hbm],
            out_specs=(vmem, vmem, vmem),
            scratch_shapes=[
                pltpu.VMEM((rows, width), BF16),
                pltpu.VMEM((n, rows, T), F32),
                pltpu.VMEM((n, rows, T), F32),
                pltpu.VMEM((2 * n, rows, T), F32),
                pltpu.VMEM((S2, rows, T), F32),
                pltpu.VMEM((S, 2, T, width), BF16),
                pltpu.VMEM((rows, width), F32),
                pltpu.VMEM((rows, width), F32),
                pltpu.VMEM((rows, LANES), F32),
                pltpu.VMEM((rows, LANES), F32),
                pltpu.VMEM((8, LANES), F32),
                pltpu.VMEM((4, 8, LANES), F32),
                pltpu.VMEM((8, LANES), F32),
                pltpu.VMEM((4, 8, LANES), F32),
                pltpu.VMEM((8, LANES), F32),
                pltpu.VMEM((8, 8, LANES), F32),
                dma((S, 2)),
                dma((S2,)),
                dma((2 * n,)),
                dma((n,)),
                dma((n,)),
                dma,
                dma,
                dma((4,)),
                dma((4,)),
                dma((4,)),
                dma((4,)),
                dma((8,)),
                dma((8,)),
            ],
            compiler_params=pltpu.CompilerParams(
                collective_id=0, has_side_effects=True, vmem_limit_bytes=52 * 2**20),
        )(hidden, lnf_gain.reshape(1, width), lnf_bias.reshape(1, width), tok_row,
          eln_gain.reshape(1, width), eln_bias.reshape(1, width), emb_table)
        logp, log_sum, next_in = pl.pallas_call(
            finish_kernel,
            out_shape=(
                jax.ShapeDtypeStruct((rows, block), F32),
                jax.ShapeDtypeStruct((1, rows), F32),
                jax.ShapeDtypeStruct((rows, width), BF16),
            ),
            in_specs=[vmem, vmem, vmem],
            out_specs=(hbm, vmem, vmem),
            scratch_shapes=[pltpu.VMEM((rows, block), F32), dma((rows // 8,))],
            compiler_params=pltpu.CompilerParams(vmem_limit_bytes=20 * 2**20),
        )(z, lse, nin)
        return logp, log_sum.reshape(rows), next_in

    return jax.shard_map(
        per_device,
        mesh=mesh,
        in_specs=(P("dp", "tp"), P("tp"), P("tp"), P("vp", "tp"), P("dp"), P("tp"), P("tp")),
        out_specs=(P("dp", ("vp", "tp")), P("dp"), P("dp", "tp")),
        check_vma=False,
    )
```

time: 382 us -> 197 us (0.52)
  waiting for transfers between devices: 234 us -> 0 us
  Pallas kernels: 0 us -> 193 us
  matrix products: 58.2 us -> 0 us
  blocking collectives: 52.3 us -> 0 us
  other arithmetic: 19.5 us -> 0 us
  between operations: 14.1 us -> 0.65 us
    reduce_scatter x1 -> x0, waiting for transfers between devices: 216 us -> none  [per_device(): lax.psum_scatter(shard_logits, 'tp', scatter_dimension=1, tiled=True)]
    pallas_call x0 -> x2, Pallas kernels: none -> 193 us  [the longest x1 189 us: per_device(): pl.pallas_call(functools.partial(logits_kernel, cfg), out_shape=(pltpu.VM...]
    dot_general x1 -> x0, matrix products: 58.2 us -> none  [per_device(): lax.dot_general(normed, emb_table, (((1,), (1,)), ((), ())), preferred_el...]
    psum x2 -> x0, blocking collectives: 30.1 us -> none  [the longest x1 24 us: global_lse(): lax.psum(jnp.sum(jnp.exp(logits - row_top[:, None]), axis=1), ('vp', 'tp'))]
    pmax x1 -> x0, blocking collectives: 22.2 us -> none  [global_lse(): row_top = lax.pmax(jnp.max(logits, axis=1), ('vp', 'tp'))]
    psum x1 -> x0, waiting for transfers between devices: 17.9 us -> none  [per_device(): tok_rows = lax.psum(picked, 'vp')]
    sub x1 -> x0, other arithmetic: 7.14 us -> none  [per_device(): logprobs = logits - log_sum[:, None]]
    reduce_sum x3 -> x0, other arithmetic: 6.46 us -> none  [the longest x1 4.49 us: global_lse(): jnp.sum(jnp.exp(logits - row_top[:, None]), axis=1)]
  transfers between devices with their start and end apart: 2 -> 0, of which waited for: 2 -> 0; matrix products, arithmetic and copies ran while one was open for 0% -> 0% of each run, Pallas kernels for 0% -> 0%
where the time goes in v1:
time: 197 us
  Pallas kernels  193 us (98%)
  local copies, waits for them, and re-layouts  2.67 us (1%)
    pallas_call x1, Pallas kernels, per_device(): pl.pallas_call(functools.partial(logits_kernel, cfg), out_shape=(pltpu.VM...  189 us
    pallas_call x1, Pallas kernels, per_device(): pl.pallas_call(finish_kernel, out_shape=(jax.ShapeDtypeStruct((rows, bloc...  4.17 us

profile of v1, /device:TPU:0, one launch (start us, length us, event | category | flops | bytes accessed | tf_op | source)
XLA Modules:
  0.0 196.7 jit_solution(9694629441244760013)
XLA Ops:
  0.6 1.2 pad.4.tok
  1.8 189.2 %shard_map.94 = (f32[64,31360]{1,0:T(8,128)S(1)}, f32[8,128]{1,0:T(8,128)}, bf16[64,512]{1,0:T(8,128)(2,1)}) custom-call(bf16[64,512]{1,0:T(8,128)(2,1)} %hid.1, f32[1,512]{1,0:T(1,128)} %bitcast.6, f32[1,512]{1,0:T(1,128)} %bitcast.7, s32[1,128]{1,0:T(1,128)} %pad.4.tok, f32[1,512]{1,0:T(1,128)} %bitcast.8, f32[1,512]{1,0:T(1,128)} %bitcast.9, ...), custom_call_target="tpu_custom_call" | custom-call | tf_op jit(solution)/shard_map/pallas_call | solution.py:308
  191.0 0.0 copy-start
  191.0 0.8 copy-done
  191.8 0.0 copy-start.1
  191.8 0.7 copy-done.1
  192.5 4.2 %shard_map.95 = (f32[64,31360]{1,0:T(8,128)}, f32[1,64]{1,0:T(1,128)}, bf16[64,512]{1,0:T(8,128)(2,1)}) custom-call(f32[64,31360]{1,0:T(8,128)S(1)} %get-tuple-element.9.z, f32[8,128]{1,0:T(8,128)S(1)} %copy-done.1, bf16[64,512]{1,0:T(8,128)(2,1)S(1)} %copy-done), custom_call_target="tpu_custom_call" | custom-call | tf_op jit(solution)/shard_map/pallas_call | solution.py:352
Async XLA Ops:
  191.0 0.8 copy-start
  191.8 0.7 copy-start.1

commit v2 on v1

--- a/solution.py
+++ b/solution.py
@@ -14,48 +14,50 @@
 LANES = 128
 
 
-def cols_to_rows(cols):
-    rows = cols[0].shape[0]
-    lane = lax.broadcasted_iota(jnp.int32, (rows, LANES), 1)
-    tile = jnp.zeros((rows, LANES), F32)
-    for k, col in enumerate(cols):
-        tile = jnp.where(lane == k, col, tile)
-    full = jnp.concatenate([tile, jnp.zeros((LANES - rows, LANES), F32)], axis=0)
-    return full.T[0:8, :]
-
-
-def rows_to_cols(tile, rows):
-    full = jnp.concatenate([tile, jnp.zeros((LANES - 8, LANES), F32)], axis=0)
-    return full.T[0:rows, :]
+def diagonal(rows):
+    return (lax.broadcasted_iota(jnp.int32, (rows, LANES), 0)
+            == lax.broadcasted_iota(jnp.int32, (rows, LANES), 1))
+
+
+def col_to_row(col):
+    return jnp.sum(jnp.where(diagonal(col.shape[0]), col, jnp.zeros_like(col)), axis=0, keepdims=True)
+
+
+def row_to_col(row, rows):
+    return jnp.sum(jnp.where(diagonal(rows), row, jnp.zeros_like(row)), axis=1, keepdims=True)
+
+
+def two_rows(first, second):
+    sub = lax.broadcasted_iota(jnp.int32, (8, LANES), 0)
+    return jnp.where(sub == 0, first, second)
 
 
 def row_sums_tile(rows_f32):
-    return cols_to_rows([
-        jnp.sum(rows_f32, axis=1, keepdims=True),
-        jnp.sum(rows_f32 * rows_f32, axis=1, keepdims=True),
-    ])
+    return two_rows(
+        col_to_row(jnp.sum(rows_f32, axis=1, keepdims=True)),
+        col_to_row(jnp.sum(rows_f32 * rows_f32, axis=1, keepdims=True)))
 
 
 def norm_rows(rows_f32, totals, gain, bias, full_width):
+    rows = rows_f32.shape[0]
     mean = totals[0:1, :] / full_width
     var = totals[1:2, :] / full_width - mean * mean
     rstd = lax.rsqrt(var + NORM_EPS)
-    pick = lax.broadcasted_iota(jnp.int32, (8, LANES), 0)
-    both = jnp.where(pick == 0, mean, rstd)
-    cols = rows_to_cols(both, rows_f32.shape[0])
-    scaled = (rows_f32 - cols[:, 0:1]) * cols[:, 1:2]
+    scaled = (rows_f32 - row_to_col(mean, rows)) * row_to_col(rstd, rows)
     return (scaled * gain + bias).astype(BF16)
 
 
 def logits_kernel(
-    cfg, hid, gain, bias, tok, egain, ebias, tab,
+    cfg, hid_hbm, gain_hbm, bias_hbm, tok_hbm, egain_hbm, ebias_hbm, tab,
     z, lse, nin,
+    hid, gain, bias, tok, egain, ebias, in_sem,
+    hds_sem, hdr_sem, hxs_sem, hxr_sem,
     xn, out, xrecv, drecv, stg, tbuf, pick, ypick, runmax, runsum,
     ln_send, ln_recv, eln_send, eln_recv, fin_send, fin_recv,
     tab_sem, dsend_sem, drecv_sem, xsend_sem, xrecv_sem, ysend_sem, yrecv_sem,
     lns_sem, lnr_sem, els_sem, elr_sem, fis_sem, fir_sem,
 ):
-    n, T, B, S, S2, n0, full_width = cfg
+    n, T, B, S, S2, n0, full_width, head = cfg
     rows = hid.shape[0]
     dp = lax.axis_index("dp")
     v = lax.axis_index("vp")
@@ -108,25 +110,36 @@
             src_ref=src, dst_ref=dst.at[d], send_sem=ssem.at[d], recv_sem=rsem.at[d],
             device_id=peer(d), device_id_type=MESH)
 
+    barrier = pltpu.get_barrier_semaphore()
+    for d in (6, 7, 5, 4, 2, 3, 1):
+        pl.semaphore_signal(barrier, inc=1, device_id=peer(d), device_id_type=MESH)
+
+    pairs = ((hid_hbm, hid), (gain_hbm, gain), (bias_hbm, bias), (tok_hbm, tok),
+             (egain_hbm, egain), (ebias_hbm, ebias))
+    loads = [pltpu.make_async_copy(src, dst, in_sem.at[k]) for k, (src, dst) in enumerate(pairs)]
+    for load in loads:
+        load.start()
     for j in range(S):
         start_table(j)
 
-    barrier = pltpu.get_barrier_semaphore()
-    for d in range(1, 8):
-        pl.semaphore_signal(barrier, inc=1, device_id=peer(d), device_id_type=MESH)
-
+    loads[0].wait()
     hid_f32 = hid[...].astype(F32)
     ln_send[...] = row_sums_tile(hid_f32)
-    tok_cols = rows_to_cols(
-        jnp.concatenate([tok[...].astype(F32), jnp.zeros((7, LANES), F32)], axis=0), rows)
-    tok_col = tok_cols[:, 0:1].astype(jnp.int32)
+    pl.semaphore_wait(barrier, 7)
+
+    for d in range(1, 4):
+        small_copy(ln_send, ln_recv, lns_sem, lnr_sem, d).start()
+    for load in loads[1:]:
+        load.wait()
+    eye = (lax.broadcasted_iota(jnp.int32, (rows, rows), 0)
+           == lax.broadcasted_iota(jnp.int32, (rows, rows), 1))
+    tok_col = jnp.sum(
+        jnp.where(eye, tok[...].astype(F32), 0.0), axis=1, keepdims=True).astype(jnp.int32)
     pick[...] = jnp.zeros_like(pick)
     runmax[...] = jnp.full(runmax.shape, -jnp.inf, F32)
     runsum[...] = jnp.zeros_like(runsum)
-    pl.semaphore_wait(barrier, 7)
-
-    for d in range(1, 4):
-        small_copy(ln_send, ln_recv, lns_sem, lnr_sem, d).start()
+    wait_table(0, 0)
+    wait_table(0, 1)
     totals = ln_send[...]
     for d in range(1, 4):
         small_copy(ln_send, ln_recv, lns_sem, lnr_sem, d).wait()
@@ -153,7 +166,7 @@
     def send_half(j):
         wait_table(j, 0)
 
-        @pl.when(j >= S2)
+        @pl.when(j > S2)
         def _():
             d2d_copy(j - S2).wait_send()
 
@@ -168,11 +181,50 @@
         def _():
             start_table(j + S)
 
-    @pl.loop(0, n)
+    def head_d2d(k):
+        cols = pl.ds(head[k], head[k + 1] - head[k])
+        return pltpu.make_async_remote_copy(
+            src_ref=stg.at[0, :, cols], dst_ref=drecv.at[0, :, cols],
+            send_sem=hds_sem.at[k], recv_sem=hdr_sem.at[k],
+            device_id=peer(1), device_id_type=MESH)
+
+    def head_x(k):
+        cols = pl.ds(head[k], head[k + 1] - head[k])
+        return pltpu.make_async_remote_copy(
+            src_ref=out.at[0, :, cols], dst_ref=xrecv.at[0, :, cols],
+            send_sem=hxs_sem.at[k], recv_sem=hxr_sem.at[k],
+            device_id=peer(2), device_id_type=MESH)
+
+    def head_matmul(k, w):
+        return lax.dot_general(
+            xn[...], tbuf[0, w, head[k]:head[k + 1], :], (((1,), (1,)), ((), ())),
+            preferred_element_type=F32)
+
+    def head_combine(k):
+        head_d2d(k).wait_recv()
+        cols = slice(head[k], head[k + 1])
+        out[0, :, cols] = out[0, :, cols] + drecv[0, :, cols]
+
+    pieces = len(head) - 1
+    for k in range(pieces):
+        stg[0, :, head[k]:head[k + 1]] = head_matmul(k, 0)
+        out[0, :, head[k]:head[k + 1]] = head_matmul(k, 1)
+        head_d2d(k).start()
+        if k >= 1:
+            head_combine(k - 1)
+            head_x(k - 1).start()
+    pick_rows(0)
+    refill(0)
+    head_combine(pieces - 1)
+    for k in range(pieces):
+        head_d2d(k).wait_send()
+    head_x(pieces - 1).start()
+
+    @pl.loop(1, n)
     def _(j):
         send_half(j)
 
-        @pl.when(j >= 1)
+        @pl.when(j >= 2)
         def _():
             combine_out(j - 1)
 
@@ -180,7 +232,7 @@
         wait_table(j, 1)
         out[j] = matmul(j, 1)
 
-        @pl.when(jnp.logical_and(j >= 1, j <= n0))
+        @pl.when(jnp.logical_and(j >= 2, j <= n0))
         def _():
             x_copy(j - 1).start()
 
@@ -221,9 +273,7 @@
     for i in range(n0, n):
         x_copy(i).start()
 
-    @pl.loop(0, n)
-    def _(i):
-        x_copy(i).wait_recv()
+    def absorb(i):
         m_old = runmax[...]
         m_new = m_old
         for k in range(T // LANES):
@@ -238,10 +288,21 @@
         runmax[...] = m_new
         runsum[...] = s_new
 
+    for k in range(pieces):
+        head_x(k).wait_recv()
+
+    @pl.loop(0, n)
+    def _(i):
+        @pl.when(i >= 1)
+        def _():
+            x_copy(i).wait_recv()
+
+        absorb(i)
+
     top = jnp.max(runmax[...], axis=1, keepdims=True)
     exp_sum = jnp.sum(runsum[...] * jnp.exp(runmax[...] - top), axis=1, keepdims=True)
-    fin_send[...] = cols_to_rows([top, exp_sum])
-    for d in range(1, 8):
+    fin_send[...] = two_rows(col_to_row(top), col_to_row(exp_sum))
+    for d in (6, 7, 5, 4, 2, 3, 1):
         small_copy(fin_send, fin_recv, fis_sem, fir_sem, d).start()
 
     totals = eln_send[...]
@@ -250,7 +311,10 @@
         totals = totals + eln_recv[d]
     nin[...] = norm_rows(pick[...] + ypick[...], totals, egain[...], ebias[...], full_width)
 
-    @pl.loop(0, n)
+    for k in range(pieces):
+        head_x(k).wait_send()
+
+    @pl.loop(1, n)
     def _(i):
         x_copy(i).wait_send()
 
@@ -271,22 +335,27 @@
     lse[...] = jnp.broadcast_to(best + jnp.log(total), lse.shape)
 
 
-def finish_kernel(z, lse, nin, logp, log_sum, next_in, buf, sem):
+def finish_kernel(z, lse, nin, logp, log_sum, next_in, buf, row, sem, small_sem):
     rows = z.shape[0]
-    col = rows_to_cols(lse[...], rows)[:, 0:1]
+    col = row_to_col(lse[0:1, :], rows)
     steps = rows // 8
 
     def put(b):
         return pltpu.make_async_copy(
             buf.at[pl.ds(8 * b, 8)], logp.at[pl.ds(8 * b, 8)], sem.at[b])
 
+    row[...] = lse[0:1, 0:rows]
+    nin_copy = pltpu.make_async_copy(nin, next_in, small_sem.at[0])
+    nin_copy.start()
     for b in range(steps):
         buf[8 * b:8 * b + 8, :] = z[8 * b:8 * b + 8, :] - col[8 * b:8 * b + 8, :]
         if b >= 1:
             put(b - 1).start()
-    next_in[...] = nin[...]
-    log_sum[...] = lse[0:1, 0:rows]
     put(steps - 1).start()
+    row_copy = pltpu.make_async_copy(row, log_sum, small_sem.at[1])
+    row_copy.start()
+    nin_copy.wait()
+    row_copy.wait()
     for b in range(steps):
         put(b).wait()
 
@@ -300,21 +369,32 @@
         T = 7 * LANES
         n = block // T
         S, S2, n0 = 3, 4, 25
-        cfg = (n, T, block, S, S2, n0, float(width * tp_size))
+        head = (0, LANES, 3 * LANES, T)
+        cfg = (n, T, block, S, S2, n0, float(width * tp_size), head)
         vmem = pl.BlockSpec(memory_space=pltpu.VMEM)
         hbm = pl.BlockSpec(memory_space=pl.ANY)
-        tok_row = jnp.pad(next_tok.reshape(1, rows), ((0, 0), (0, LANES - rows)))
         dma = pltpu.SemaphoreType.DMA
         z, lse, nin = pl.pallas_call(
             functools.partial(logits_kernel, cfg),
             out_shape=(
                 pltpu.VMEM((rows, block), F32),
-                jax.ShapeDtypeStruct((8, LANES), F32),
-                jax.ShapeDtypeStruct((rows, width), BF16),
+                pltpu.VMEM((8, LANES), F32),
+                pltpu.VMEM((rows, width), BF16),
             ),
-            in_specs=[vmem] * 6 + [hbm],
+            in_specs=[hbm] * 7,
             out_specs=(vmem, vmem, vmem),
             scratch_shapes=[
+                pltpu.VMEM((rows, width), BF16),
+                pltpu.VMEM((1, width), F32),
+                pltpu.VMEM((1, width), F32),
+                pltpu.VMEM((1, rows), jnp.int32),
+                pltpu.VMEM((1, width), F32),
+                pltpu.VMEM((1, width), F32),
+                dma((6,)),
+                dma((3,)),
+                dma((3,)),
+                dma((3,)),
+                dma((3,)),
                 pltpu.VMEM((rows, width), BF16),
                 pltpu.VMEM((n, rows, T), F32),
                 pltpu.VMEM((n, rows, T), F32),
@@ -347,7 +427,7 @@
             ],
             compiler_params=pltpu.CompilerParams(
                 collective_id=0, has_side_effects=True, vmem_limit_bytes=52 * 2**20),
-        )(hidden, lnf_gain.reshape(1, width), lnf_bias.reshape(1, width), tok_row,
+        )(hidden, lnf_gain.reshape(1, width), lnf_bias.reshape(1, width), next_tok.reshape(1, rows),
           eln_gain.reshape(1, width), eln_bias.reshape(1, width), emb_table)
         logp, log_sum, next_in = pl.pallas_call(
             finish_kernel,
@@ -357,8 +437,9 @@
                 jax.ShapeDtypeStruct((rows, width), BF16),
             ),
             in_specs=[vmem, vmem, vmem],
-            out_specs=(hbm, vmem, vmem),
-            scratch_shapes=[pltpu.VMEM((rows, block), F32), dma((rows // 8,))],
+            out_specs=(hbm, hbm, hbm),
+            scratch_shapes=[
+                pltpu.VMEM((rows, block), F32), pltpu.VMEM((1, rows), F32), dma((rows // 8,)), dma((2,))],
             compiler_params=pltpu.CompilerParams(vmem_limit_bytes=20 * 2**20),
         )(z, lse, nin)
         return logp, log_sum.reshape(rows), next_in

time: 197 us -> 191 us (0.970)
  local copies, waits for them, and re-layouts: 2.67 us -> 0 us
  Pallas kernels: 193 us -> 191 us
    pallas_call x1, Pallas kernels: 189 us -> 187 us  [per_device(): pl.pallas_call(functools.partial(logits_kernel, cfg), out_shape=(pltpu.VM...]
where the time goes in v2:
time: 191 us
  Pallas kernels  191 us (100%)
    pallas_call x1, Pallas kernels, per_device(): pl.pallas_call(functools.partial(logits_kernel, cfg), out_shape=(pltpu.VM...  187 us

profile of v2, /device:TPU:0, one launch (start us, length us, event | category | flops | bytes accessed | tf_op | source)
XLA Modules:
  0.0 191.3 jit_solution(9481432937116198355)
XLA Ops:
  0.6 187.1 %shard_map.94 = (f32[64,31360]{1,0:T(8,128)S(1)}, f32[8,128]{1,0:T(8,128)S(1)}, bf16[64,512]{1,0:T(8,128)(2,1)S(1)}) custom-call(bf16[64,512]{1,0:T(8,128)(2,1)} %hid_hbm.1, f32[1,512]{1,0:T(1,128)} %bitcast.6, f32[1,512]{1,0:T(1,128)} %bitcast.7, s32[1,64]{1,0:T(1,128)} %bitcast.10, f32[1,512]{1,0:T(1,128)} %bitcast.8, f32[1,512]{1,0:T(1,128)} %bitcast.9, ...), custom_call_target="tpu_custom_call" | custom-call | tf_op jit(solution)/shard_map/pallas_call | solution.py:377
  187.8 3.5 %shard_map.95 = (f32[64,31360]{1,0:T(8,128)}, f32[1,64]{1,0:T(1,128)}, bf16[64,512]{1,0:T(8,128)(2,1)}) custom-call(f32[64,31360]{1,0:T(8,128)S(1)} %get-tuple-element.9.z, f32[8,128]{1,0:T(8,128)S(1)} %get-tuple-element.10.lse, bf16[64,512]{1,0:T(8,128)(2,1)S(1)} %get-tuple-element.11.nin), custom_call_target="tpu_custom_call" | custom-call | tf_op jit(solution)/shard_map/pallas_call | solution.py:432

commit v3 on v2

--- a/solution.py
+++ b/solution.py
@@ -51,13 +51,13 @@
     cfg, hid_hbm, gain_hbm, bias_hbm, tok_hbm, egain_hbm, ebias_hbm, tab,
     z, lse, nin,
     hid, gain, bias, tok, egain, ebias, in_sem,
-    hds_sem, hdr_sem, hxs_sem, hxr_sem,
+    hds_sem, hdr_sem, hxr_sem,
     xn, out, xrecv, drecv, stg, tbuf, pick, ypick, runmax, runsum,
     ln_send, ln_recv, eln_send, eln_recv, fin_send, fin_recv,
     tab_sem, dsend_sem, drecv_sem, xsend_sem, xrecv_sem, ysend_sem, yrecv_sem,
     lns_sem, lnr_sem, els_sem, elr_sem, fis_sem, fir_sem,
 ):
-    n, T, B, S, S2, n0, full_width, head = cfg
+    n, T, B, S, S2, n0, full_width, head, groups = cfg
     rows = hid.shape[0]
     dp = lax.axis_index("dp")
     v = lax.axis_index("vp")
@@ -79,11 +79,11 @@
             cc = 1 - c if w == 0 else c
             row = pl.multiple_of((2 * xx + cc) * B + i * T, LANES)
             slot = lax.rem(j, S)
-            pltpu.make_async_copy(tab.at[pl.ds(row, T)], tbuf.at[slot, w], tab_sem.at[slot, w]).start()
-
-    def wait_table(j, w):
+            pltpu.make_async_copy(tab.at[pl.ds(row, T)], tbuf.at[slot, w], tab_sem.at[slot]).start()
+
+    def wait_table(j):
         slot = lax.rem(j, S)
-        pltpu.make_async_copy(tab.at[pl.ds(0, T)], tbuf.at[slot, w], tab_sem.at[slot, w]).wait()
+        pltpu.make_async_copy(tbuf.at[slot], tbuf.at[slot], tab_sem.at[slot]).wait()
 
     def first_row(j, w):
         a = lax.div(j, n)
@@ -95,23 +95,32 @@
     def d2d_copy(j):
         slot = lax.rem(j, S2)
         return pltpu.make_async_remote_copy(
-            src_ref=stg.at[slot], dst_ref=drecv.at[j],
-            send_sem=dsend_sem.at[slot], recv_sem=drecv_sem.at[j],
+            src_ref=stg.at[slot], dst_ref=drecv.at[slot],
+            send_sem=dsend_sem.at[slot], recv_sem=drecv_sem.at[slot],
             device_id=peer(1), device_id_type=MESH)
 
-    def x_copy(i):
+    def x_copy(g):
+        first, last = groups[g]
+        part = pl.ds(first, last - first)
         return pltpu.make_async_remote_copy(
-            src_ref=out.at[i], dst_ref=xrecv.at[i],
-            send_sem=xsend_sem.at[i], recv_sem=xrecv_sem.at[i],
+            src_ref=out.at[part], dst_ref=xrecv.at[part],
+            send_sem=xsend_sem, recv_sem=xrecv_sem.at[g],
             device_id=peer(2), device_id_type=MESH)
 
     def small_copy(src, dst, ssem, rsem, d):
         return pltpu.make_async_remote_copy(
-            src_ref=src, dst_ref=dst.at[d], send_sem=ssem.at[d], recv_sem=rsem.at[d],
+            src_ref=src, dst_ref=dst.at[d - 1], send_sem=ssem, recv_sem=rsem,
             device_id=peer(d), device_id_type=MESH)
 
+    def wait_small(dst, ssem, rsem):
+        both = pltpu.make_async_remote_copy(
+            src_ref=dst, dst_ref=dst, send_sem=ssem, recv_sem=rsem,
+            device_id=peer(1), device_id_type=MESH)
+        both.wait_recv()
+        both.wait_send()
+
     barrier = pltpu.get_barrier_semaphore()
-    for d in (6, 7, 5, 4, 2, 3, 1):
+    for d in (4, 2, 3, 1):
         pl.semaphore_signal(barrier, inc=1, device_id=peer(d), device_id_type=MESH)
 
     pairs = ((hid_hbm, hid), (gain_hbm, gain), (bias_hbm, bias), (tok_hbm, tok),
@@ -125,9 +134,9 @@
     loads[0].wait()
     hid_f32 = hid[...].astype(F32)
     ln_send[...] = row_sums_tile(hid_f32)
-    pl.semaphore_wait(barrier, 7)
-
-    for d in range(1, 4):
+    pl.semaphore_wait(barrier, 4)
+
+    for d in (2, 3, 1):
         small_copy(ln_send, ln_recv, lns_sem, lnr_sem, d).start()
     for load in loads[1:]:
         load.wait()
@@ -138,11 +147,10 @@
     pick[...] = jnp.zeros_like(pick)
     runmax[...] = jnp.full(runmax.shape, -jnp.inf, F32)
     runsum[...] = jnp.zeros_like(runsum)
-    wait_table(0, 0)
-    wait_table(0, 1)
+    wait_table(0)
     totals = ln_send[...]
-    for d in range(1, 4):
-        small_copy(ln_send, ln_recv, lns_sem, lnr_sem, d).wait()
+    wait_small(ln_recv, lns_sem, lnr_sem)
+    for d in range(3):
         totals = totals + ln_recv[d]
     xn[...] = norm_rows(hid_f32, totals, gain[...], bias[...], full_width)
 
@@ -164,7 +172,7 @@
         return pl.ds(pl.multiple_of(i * T, LANES), T)
 
     def send_half(j):
-        wait_table(j, 0)
+        wait_table(j)
 
         @pl.when(j > S2)
         def _():
@@ -174,7 +182,7 @@
 
     def combine_out(i):
         d2d_copy(i).wait_recv()
-        out[i] = out[i] + drecv[i]
+        out[i] = out[i] + drecv[lax.rem(i, S2)]
 
     def refill(j):
         @pl.when(j + S < 2 * n)
@@ -192,7 +200,7 @@
         cols = pl.ds(head[k], head[k + 1] - head[k])
         return pltpu.make_async_remote_copy(
             src_ref=out.at[0, :, cols], dst_ref=xrecv.at[0, :, cols],
-            send_sem=hxs_sem.at[k], recv_sem=hxr_sem.at[k],
+            send_sem=xsend_sem, recv_sem=hxr_sem,
             device_id=peer(2), device_id_type=MESH)
 
     def head_matmul(k, w):
@@ -206,19 +214,48 @@
         out[0, :, cols] = out[0, :, cols] + drecv[0, :, cols]
 
     pieces = len(head) - 1
-    for k in range(pieces):
+
+    def head_give(k):
         stg[0, :, head[k]:head[k + 1]] = head_matmul(k, 0)
+
+    def head_keep(k):
         out[0, :, head[k]:head[k + 1]] = head_matmul(k, 1)
-        head_d2d(k).start()
-        if k >= 1:
+
+    @pl.when(c == 0)
+    def _():
+        for k in range(pieces):
+            head_keep(k)
+        for k in range(pieces):
+            head_give(k)
+            head_combine(k)
+            head_d2d(k).start()
+            if k >= 1:
+                head_x(k - 1).start()
+        pick_rows(0)
+        head_x(pieces - 1).start()
+
+    @pl.when(c == 1)
+    def _():
+        head_give(0)
+        for k in range(pieces):
+            if k + 1 < pieces:
+                head_give(k + 1)
+            else:
+                head_keep(0)
+            head_d2d(k).start()
+        for k in range(1, pieces):
+            head_keep(k)
             head_combine(k - 1)
-            head_x(k - 1).start()
-    pick_rows(0)
+            if k >= 2:
+                head_x(k - 2).start()
+        head_x(pieces - 2).start()
+        pick_rows(0)
+        head_combine(pieces - 1)
+        head_x(pieces - 1).start()
+
     refill(0)
-    head_combine(pieces - 1)
     for k in range(pieces):
         head_d2d(k).wait_send()
-    head_x(pieces - 1).start()
 
     @pl.loop(1, n)
     def _(j):
@@ -229,12 +266,12 @@
             combine_out(j - 1)
 
         d2d_copy(j).start()
-        wait_table(j, 1)
         out[j] = matmul(j, 1)
 
-        @pl.when(jnp.logical_and(j >= 2, j <= n0))
-        def _():
-            x_copy(j - 1).start()
+        for g in range(n0):
+            @pl.when(j == groups[g][1])
+            def _():
+                x_copy(g).start()
 
         pick_rows(j)
         refill(j)
@@ -250,16 +287,15 @@
         @pl.when(j > n)
         def _():
             d2d_copy(j - 1).wait_recv()
-            z[:, zcols(j - 1 - n)] = z[:, zcols(j - 1 - n)] + drecv[j - 1]
+            z[:, zcols(j - 1 - n)] = z[:, zcols(j - 1 - n)] + drecv[lax.rem(j - 1, S2)]
 
         d2d_copy(j).start()
-        wait_table(j, 1)
         z[:, zcols(j - n)] = matmul(j, 1)
         pick_rows(j)
         refill(j)
 
     d2d_copy(2 * n - 1).wait_recv()
-    z[:, zcols(n - 1)] = z[:, zcols(n - 1)] + drecv[2 * n - 1]
+    z[:, zcols(n - 1)] = z[:, zcols(n - 1)] + drecv[(2 * n - 1) % S2]
 
     ycopy = pltpu.make_async_remote_copy(
         src_ref=pick, dst_ref=ypick, send_sem=ysend_sem, recv_sem=yrecv_sem,
@@ -270,8 +306,8 @@
     eln_send[...] = row_sums_tile(tok_rows)
     for d in range(1, 4):
         small_copy(eln_send, eln_recv, els_sem, elr_sem, d).start()
-    for i in range(n0, n):
-        x_copy(i).start()
+    for g in range(n0, len(groups)):
+        x_copy(g).start()
 
     def absorb(i):
         m_old = runmax[...]
@@ -288,16 +324,17 @@
         runmax[...] = m_new
         runsum[...] = s_new
 
-    for k in range(pieces):
-        head_x(k).wait_recv()
-
-    @pl.loop(0, n)
-    def _(i):
-        @pl.when(i >= 1)
-        def _():
-            x_copy(i).wait_recv()
-
-        absorb(i)
+    pltpu.make_async_remote_copy(
+        src_ref=out.at[0], dst_ref=xrecv.at[0], send_sem=xsend_sem, recv_sem=hxr_sem,
+        device_id=peer(2), device_id_type=MESH).wait_recv()
+
+    absorb(0)
+    for g, (first, last) in enumerate(groups):
+        x_copy(g).wait_recv()
+
+        @pl.loop(first, last)
+        def _(i):
+            absorb(i)
 
     top = jnp.max(runmax[...], axis=1, keepdims=True)
     exp_sum = jnp.sum(runsum[...] * jnp.exp(runmax[...] - top), axis=1, keepdims=True)
@@ -306,25 +343,22 @@
         small_copy(fin_send, fin_recv, fis_sem, fir_sem, d).start()
 
     totals = eln_send[...]
-    for d in range(1, 4):
-        small_copy(eln_send, eln_recv, els_sem, elr_sem, d).wait()
+    wait_small(eln_recv, els_sem, elr_sem)
+    for d in range(3):
         totals = totals + eln_recv[d]
     nin[...] = norm_rows(pick[...] + ypick[...], totals, egain[...], ebias[...], full_width)
 
-    for k in range(pieces):
-        head_x(k).wait_send()
-
-    @pl.loop(1, n)
-    def _(i):
-        x_copy(i).wait_send()
+    pltpu.make_async_remote_copy(
+        src_ref=out, dst_ref=xrecv, send_sem=xsend_sem, recv_sem=hxr_sem,
+        device_id=peer(2), device_id_type=MESH).wait_send()
 
     @pl.loop(2 * n - S2, 2 * n)
     def _(j):
         d2d_copy(j).wait_send()
 
     tiles = [fin_send[...]]
-    for d in range(1, 8):
-        small_copy(fin_send, fin_recv, fis_sem, fir_sem, d).wait()
+    wait_small(fin_recv, fis_sem, fir_sem)
+    for d in range(7):
         tiles.append(fin_recv[d])
     best = tiles[0][0:1, :]
     for tile in tiles[1:]:
@@ -336,28 +370,31 @@
 
 
 def finish_kernel(z, lse, nin, logp, log_sum, next_in, buf, row, sem, small_sem):
-    rows = z.shape[0]
+    rows, width = z.shape
     col = row_to_col(lse[0:1, :], rows)
-    steps = rows // 8
+    cuts = [0, 16 * LANES, 48 * LANES, 112 * LANES, width]
+    parts = [(0, lo, hi) for lo, hi in zip(cuts, cuts[1:])]
+    parts += [(r, 0, width) for r in range(8, rows, 8)]
 
     def put(b):
-        return pltpu.make_async_copy(
-            buf.at[pl.ds(8 * b, 8)], logp.at[pl.ds(8 * b, 8)], sem.at[b])
+        r, lo, hi = parts[b]
+        part = (pl.ds(r, 8), pl.ds(lo, hi - lo))
+        return pltpu.make_async_copy(buf.at[part], logp.at[part], sem)
 
     row[...] = lse[0:1, 0:rows]
     nin_copy = pltpu.make_async_copy(nin, next_in, small_sem.at[0])
-    nin_copy.start()
-    for b in range(steps):
-        buf[8 * b:8 * b + 8, :] = z[8 * b:8 * b + 8, :] - col[8 * b:8 * b + 8, :]
+    row_copy = pltpu.make_async_copy(row, log_sum, small_sem.at[1])
+    for b, (r, lo, hi) in enumerate(parts):
+        buf[r:r + 8, lo:hi] = z[r:r + 8, lo:hi] - col[r:r + 8, :]
         if b >= 1:
             put(b - 1).start()
-    put(steps - 1).start()
-    row_copy = pltpu.make_async_copy(row, log_sum, small_sem.at[1])
-    row_copy.start()
+        if b == 3:
+            nin_copy.start()
+            row_copy.start()
+    put(len(parts) - 1).start()
     nin_copy.wait()
     row_copy.wait()
-    for b in range(steps):
-        put(b).wait()
+    pltpu.make_async_copy(buf, logp, sem).wait()
 
 
 def solution(mesh):
@@ -368,9 +405,14 @@
         block = emb_table.shape[0] // tp_size
         T = 7 * LANES
         n = block // T
-        S, S2, n0 = 3, 4, 25
+        S, S2, n0 = 3, 4, 8
+        sizes = (1, 1, 2, 5, 5, 5, 5, 5, 2, 2, 1)
+        groups, at = [], 1
+        for size in sizes:
+            groups.append((at, at + size))
+            at += size
         head = (0, LANES, 3 * LANES, T)
-        cfg = (n, T, block, S, S2, n0, float(width * tp_size), head)
+        cfg = (n, T, block, S, S2, n0, float(width * tp_size), head, tuple(groups))
         vmem = pl.BlockSpec(memory_space=pltpu.VMEM)
         hbm = pl.BlockSpec(memory_space=pl.ANY)
         dma = pltpu.SemaphoreType.DMA
@@ -393,12 +435,11 @@
                 dma((6,)),
                 dma((3,)),
                 dma((3,)),
-                dma((3,)),
-                dma((3,)),
+                dma,
                 pltpu.VMEM((rows, width), BF16),
                 pltpu.VMEM((n, rows, T), F32),
                 pltpu.VMEM((n, rows, T), F32),
-                pltpu.VMEM((2 * n, rows, T), F32),
+                pltpu.VMEM((S2, rows, T), F32),
                 pltpu.VMEM((S2, rows, T), F32),
                 pltpu.VMEM((S, 2, T, width), BF16),
                 pltpu.VMEM((rows, width), F32),
@@ -406,24 +447,24 @@
                 pltpu.VMEM((rows, LANES), F32),
                 pltpu.VMEM((rows, LANES), F32),
                 pltpu.VMEM((8, LANES), F32),
-                pltpu.VMEM((4, 8, LANES), F32),
+                pltpu.VMEM((3, 8, LANES), F32),
                 pltpu.VMEM((8, LANES), F32),
-                pltpu.VMEM((4, 8, LANES), F32),
+                pltpu.VMEM((3, 8, LANES), F32),
                 pltpu.VMEM((8, LANES), F32),
-                pltpu.VMEM((8, 8, LANES), F32),
-                dma((S, 2)),
+                pltpu.VMEM((7, 8, LANES), F32),
+                dma((S,)),
                 dma((S2,)),
-                dma((2 * n,)),
-                dma((n,)),
-                dma((n,)),
-                dma,
-                dma,
-                dma((4,)),
-                dma((4,)),
-                dma((4,)),
-                dma((4,)),
-                dma((8,)),
-                dma((8,)),
+                dma((S2,)),
+                dma,
+                dma((len(groups),)),
+                dma,
+                dma,
+                dma,
+                dma,
+                dma,
+                dma,
+                dma,
+                dma,
             ],
             compiler_params=pltpu.CompilerParams(
                 collective_id=0, has_side_effects=True, vmem_limit_bytes=52 * 2**20),
@@ -439,7 +480,7 @@
             in_specs=[vmem, vmem, vmem],
             out_specs=(hbm, hbm, hbm),
             scratch_shapes=[
-                pltpu.VMEM((rows, block), F32), pltpu.VMEM((1, rows), F32), dma((rows // 8,)), dma((2,))],
+                pltpu.VMEM((rows, block), F32), pltpu.VMEM((1, rows), F32), dma, dma((2,))],
             compiler_params=pltpu.CompilerParams(vmem_limit_bytes=20 * 2**20),
         )(z, lse, nin)
         return logp, log_sum.reshape(rows), next_in

time: 191 us -> 190 us (level)
  Pallas kernels: 191 us -> 189 us
where the time goes in v3:
time: 190 us
  Pallas kernels  189 us (99%)
    pallas_call x1, Pallas kernels, per_device(): pl.pallas_call(functools.partial(logits_kernel, cfg), out_shape=(pltpu.VM...  186 us

profile of v3, /device:TPU:0, one launch (start us, length us, event | category | flops | bytes accessed | tf_op | source)
XLA Modules:
  0.0 189.8 jit_solution(14305950626535385636)
XLA Ops:
  0.6 185.9 %shard_map.94 = (f32[64,31360]{1,0:T(8,128)S(1)}, f32[8,128]{1,0:T(8,128)S(1)}, bf16[64,512]{1,0:T(8,128)(2,1)S(1)}) custom-call(bf16[64,512]{1,0:T(8,128)(2,1)} %hid_hbm.1, f32[1,512]{1,0:T(1,128)} %bitcast.6, f32[1,512]{1,0:T(1,128)} %bitcast.7, s32[1,64]{1,0:T(1,128)} %bitcast.10, f32[1,512]{1,0:T(1,128)} %bitcast.8, f32[1,512]{1,0:T(1,128)} %bitcast.9, ...), custom_call_target="tpu_custom_call" | custom-call | tf_op jit(solution)/shard_map/pallas_call | solution.py:419
  186.5 3.3 %shard_map.95 = (f32[64,31360]{1,0:T(8,128)}, f32[1,64]{1,0:T(1,128)}, bf16[64,512]{1,0:T(8,128)(2,1)}) custom-call(f32[64,31360]{1,0:T(8,128)S(1)} %get-tuple-element.9.z, f32[8,128]{1,0:T(8,128)S(1)} %get-tuple-element.10.lse, bf16[64,512]{1,0:T(8,128)(2,1)S(1)} %get-tuple-element.11.nin), custom_call_target="tpu_custom_call" | custom-call | tf_op jit(solution)/shard_map/pallas_call | solution.py:473

commit v4 on v3

--- a/solution.py
+++ b/solution.py
@@ -193,7 +193,7 @@
         cols = pl.ds(head[k], head[k + 1] - head[k])
         return pltpu.make_async_remote_copy(
             src_ref=stg.at[0, :, cols], dst_ref=drecv.at[0, :, cols],
-            send_sem=hds_sem.at[k], recv_sem=hdr_sem.at[k],
+            send_sem=hds_sem, recv_sem=hdr_sem.at[k],
             device_id=peer(1), device_id_type=MESH)
 
     def head_x(k):
@@ -225,54 +225,55 @@
     def _():
         for k in range(pieces):
             head_keep(k)
+        head_give(0)
+        for k in range(pieces):
+            head_combine(k)
+            if k + 1 < pieces:
+                head_give(k + 1)
+            head_d2d(k).start()
+            head_x(k).start()
+        pick_rows(0)
+
+    @pl.when(c == 1)
+    def _():
         for k in range(pieces):
             head_give(k)
-            head_combine(k)
-            head_d2d(k).start()
             if k >= 1:
-                head_x(k - 1).start()
-        pick_rows(0)
-        head_x(pieces - 1).start()
-
-    @pl.when(c == 1)
-    def _():
-        head_give(0)
-        for k in range(pieces):
-            if k + 1 < pieces:
-                head_give(k + 1)
-            else:
-                head_keep(0)
-            head_d2d(k).start()
+                head_d2d(k - 1).start()
+        head_keep(0)
+        head_d2d(pieces - 1).start()
         for k in range(1, pieces):
             head_keep(k)
-            head_combine(k - 1)
-            if k >= 2:
-                head_x(k - 2).start()
-        head_x(pieces - 2).start()
         pick_rows(0)
-        head_combine(pieces - 1)
-        head_x(pieces - 1).start()
+        for k in range(pieces):
+            head_combine(k)
 
     refill(0)
-    for k in range(pieces):
-        head_d2d(k).wait_send()
+    pltpu.make_async_remote_copy(
+        src_ref=stg.at[0], dst_ref=drecv.at[0], send_sem=hds_sem, recv_sem=hdr_sem.at[0],
+        device_id=peer(1), device_id_type=MESH).wait_send()
 
     @pl.loop(1, n)
     def _(j):
+        @pl.when(jnp.logical_and(c == 1, j == 2))
+        def _():
+            for k in range(pieces):
+                head_x(k).start()
+
+        @pl.when(j >= 2)
+        def _():
+            combine_out(j - 1)
+
         send_half(j)
-
-        @pl.when(j >= 2)
-        def _():
-            combine_out(j - 1)
-
-        d2d_copy(j).start()
-        out[j] = matmul(j, 1)
 
         for g in range(n0):
             @pl.when(j == groups[g][1])
             def _():
                 x_copy(g).start()
 
+        d2d_copy(j).start()
+
+        out[j] = matmul(j, 1)
         pick_rows(j)
         refill(j)
 
@@ -405,8 +406,8 @@
         block = emb_table.shape[0] // tp_size
         T = 7 * LANES
         n = block // T
-        S, S2, n0 = 3, 4, 8
-        sizes = (1, 1, 2, 5, 5, 5, 5, 5, 2, 2, 1)
+        S, S2, n0 = 3, 3, 5
+        sizes = (1, 2, 5, 10, 10, 5, 1)
         groups, at = [], 1
         for size in sizes:
             groups.append((at, at + size))
@@ -433,8 +434,8 @@
                 pltpu.VMEM((1, width), F32),
                 pltpu.VMEM((1, width), F32),
                 dma((6,)),
-                dma((3,)),
-                dma((3,)),
+                dma,
+                dma((len(head) - 1,)),
                 dma,
                 pltpu.VMEM((rows, width), BF16),
                 pltpu.VMEM((n, rows, T), F32),

time: 190 us -> 190 us (level)
  no operation moved by 1% of the time
where the time goes in v4:
time: 190 us; the launch traced here: 189 us
  Pallas kernels  189 us (99%)
    pallas_call x1, Pallas kernels, per_device(): pl.pallas_call(functools.partial(logits_kernel, cfg), out_shape=(pltpu.VM...  185 us

profile of v4, /device:TPU:0, one launch (start us, length us, event | category | flops | bytes accessed | tf_op | source)
XLA Modules:
  0.0 189.4 jit_solution(859235839839832970)
XLA Ops:
  0.6 185.5 %shard_map.94 = (f32[64,31360]{1,0:T(8,128)S(1)}, f32[8,128]{1,0:T(8,128)S(1)}, bf16[64,512]{1,0:T(8,128)(2,1)S(1)}) custom-call(bf16[64,512]{1,0:T(8,128)(2,1)} %hid_hbm.1, f32[1,512]{1,0:T(1,128)} %bitcast.6, f32[1,512]{1,0:T(1,128)} %bitcast.7, s32[1,64]{1,0:T(1,128)} %bitcast.10, f32[1,512]{1,0:T(1,128)} %bitcast.8, f32[1,512]{1,0:T(1,128)} %bitcast.9, ...), custom_call_target="tpu_custom_call" | custom-call | tf_op jit(solution)/shard_map/pallas_call | solution.py:420
  186.1 3.3 %shard_map.95 = (f32[64,31360]{1,0:T(8,128)}, f32[1,64]{1,0:T(1,128)}, bf16[64,512]{1,0:T(8,128)(2,1)}) custom-call(f32[64,31360]{1,0:T(8,128)S(1)} %get-tuple-element.9.z, f32[8,128]{1,0:T(8,128)S(1)} %get-tuple-element.10.lse, bf16[64,512]{1,0:T(8,128)(2,1)S(1)} %get-tuple-element.11.nin), custom_call_target="tpu_custom_call" | custom-call | tf_op jit(solution)/shard_map/pallas_call | solution.py:474

commit v5 on v4

--- a/solution.py
+++ b/solution.py
@@ -51,7 +51,7 @@
     cfg, hid_hbm, gain_hbm, bias_hbm, tok_hbm, egain_hbm, ebias_hbm, tab,
     z, lse, nin,
     hid, gain, bias, tok, egain, ebias, in_sem,
-    hds_sem, hdr_sem, hxr_sem,
+    hds_sem, hdr_sem, hxr_sem, extra, extra_sem,
     xn, out, xrecv, drecv, stg, tbuf, pick, ypick, runmax, runsum,
     ln_send, ln_recv, eln_send, eln_recv, fin_send, fin_recv,
     tab_sem, dsend_sem, drecv_sem, xsend_sem, xrecv_sem, ysend_sem, yrecv_sem,
@@ -221,25 +221,34 @@
     def head_keep(k):
         out[0, :, head[k]:head[k + 1]] = head_matmul(k, 1)
 
+    part_copy = pltpu.make_async_remote_copy(
+        src_ref=stg.at[0, :, pl.ds(head[0], head[1])], dst_ref=extra,
+        send_sem=hds_sem, recv_sem=extra_sem, device_id=peer(3), device_id_type=MESH)
+
     @pl.when(c == 0)
     def _():
-        for k in range(pieces):
+        head_keep(0)
+        head_keep(1)
+        head_x(0).start()
+        for k in range(2, pieces):
             head_keep(k)
         head_give(0)
-        for k in range(pieces):
+        for k in range(1, pieces):
             head_combine(k)
-            if k + 1 < pieces:
-                head_give(k + 1)
-            head_d2d(k).start()
+            head_give(k)
+            head_d2d(k - 1).start()
             head_x(k).start()
+        head_d2d(pieces - 1).start()
         pick_rows(0)
 
     @pl.when(c == 1)
     def _():
-        for k in range(pieces):
+        head_give(0)
+        head_give(1)
+        part_copy.start()
+        for k in range(2, pieces):
             head_give(k)
-            if k >= 1:
-                head_d2d(k - 1).start()
+            head_d2d(k - 1).start()
         head_keep(0)
         head_d2d(pieces - 1).start()
         for k in range(1, pieces):
@@ -255,11 +264,6 @@
 
     @pl.loop(1, n)
     def _(j):
-        @pl.when(jnp.logical_and(c == 1, j == 2))
-        def _():
-            for k in range(pieces):
-                head_x(k).start()
-
         @pl.when(j >= 2)
         def _():
             combine_out(j - 1)
@@ -272,6 +276,11 @@
                 x_copy(g).start()
 
         d2d_copy(j).start()
+
+        @pl.when(jnp.logical_and(c == 1, j == 1))
+        def _():
+            for k in range(pieces):
+                head_x(k).start()
 
         out[j] = matmul(j, 1)
         pick_rows(j)
@@ -329,6 +338,11 @@
         src_ref=out.at[0], dst_ref=xrecv.at[0], send_sem=xsend_sem, recv_sem=hxr_sem,
         device_id=peer(2), device_id_type=MESH).wait_recv()
 
+    @pl.when(c == 0)
+    def _():
+        part_copy.wait_recv()
+        xrecv[0, :, head[0]:head[1]] = xrecv[0, :, head[0]:head[1]] + extra[...]
+
     absorb(0)
     for g, (first, last) in enumerate(groups):
         x_copy(g).wait_recv()
@@ -412,7 +426,7 @@
         for size in sizes:
             groups.append((at, at + size))
             at += size
-        head = (0, LANES, 3 * LANES, T)
+        head = (0, 2 * LANES, 4 * LANES, T)
         cfg = (n, T, block, S, S2, n0, float(width * tp_size), head, tuple(groups))
         vmem = pl.BlockSpec(memory_space=pltpu.VMEM)
         hbm = pl.BlockSpec(memory_space=pl.ANY)
@@ -437,6 +451,8 @@
                 dma,
                 dma((len(head) - 1,)),
                 dma,
+                pltpu.VMEM((rows, head[1]), F32),
+                dma,
                 pltpu.VMEM((rows, width), BF16),
                 pltpu.VMEM((n, rows, T), F32),
                 pltpu.VMEM((n, rows, T), F32),

time: 190 us -> 189 us (level)
  no operation moved by 1% of the time
where the time goes in v5:
time: 189 us
  Pallas kernels  189 us (100%)
    pallas_call x1, Pallas kernels, per_device(): pl.pallas_call(functools.partial(logits_kernel, cfg), out_shape=(pltpu.VM...  185 us

profile of v5, /device:TPU:0, one launch (start us, length us, event | category | flops | bytes accessed | tf_op | source)
XLA Modules:
  0.0 189.3 jit_solution(14571816748943081891)
XLA Ops:
  0.6 185.3 %shard_map.94 = (f32[64,31360]{1,0:T(8,128)S(1)}, f32[8,128]{1,0:T(8,128)S(1)}, bf16[64,512]{1,0:T(8,128)(2,1)S(1)}) custom-call(bf16[64,512]{1,0:T(8,128)(2,1)} %hid_hbm.1, f32[1,512]{1,0:T(1,128)} %bitcast.6, f32[1,512]{1,0:T(1,128)} %bitcast.7, s32[1,64]{1,0:T(1,128)} %bitcast.10, f32[1,512]{1,0:T(1,128)} %bitcast.8, f32[1,512]{1,0:T(1,128)} %bitcast.9, ...), custom_call_target="tpu_custom_call" | custom-call | tf_op jit(solution)/shard_map/pallas_call | solution.py:434
  185.9 3.3 %shard_map.95 = (f32[64,31360]{1,0:T(8,128)}, f32[1,64]{1,0:T(1,128)}, bf16[64,512]{1,0:T(8,128)(2,1)}) custom-call(f32[64,31360]{1,0:T(8,128)S(1)} %get-tuple-element.9.z, f32[8,128]{1,0:T(8,128)S(1)} %get-tuple-element.10.lse, bf16[64,512]{1,0:T(8,128)(2,1)S(1)} %get-tuple-element.11.nin), custom_call_target="tpu_custom_call" | custom-call | tf_op jit(solution)/shard_map/pallas_call | solution.py:490

commit v6 on v5

--- a/solution.py
+++ b/solution.py
@@ -279,8 +279,9 @@
 
         @pl.when(jnp.logical_and(c == 1, j == 1))
         def _():
-            for k in range(pieces):
-                head_x(k).start()
+            pltpu.make_async_remote_copy(
+                src_ref=out.at[0], dst_ref=xrecv.at[0], send_sem=xsend_sem, recv_sem=hxr_sem,
+                device_id=peer(2), device_id_type=MESH).start()
 
         out[j] = matmul(j, 1)
         pick_rows(j)
@@ -387,9 +388,8 @@
 def finish_kernel(z, lse, nin, logp, log_sum, next_in, buf, row, sem, small_sem):
     rows, width = z.shape
     col = row_to_col(lse[0:1, :], rows)
-    cuts = [0, 16 * LANES, 48 * LANES, 112 * LANES, width]
-    parts = [(0, lo, hi) for lo, hi in zip(cuts, cuts[1:])]
-    parts += [(r, 0, width) for r in range(8, rows, 8)]
+    piece = 49 * LANES
+    parts = [(r, lo, lo + piece) for r in range(0, rows, 8) for lo in range(0, width, piece)]
 
     def put(b):
         r, lo, hi = parts[b]
@@ -402,8 +402,8 @@
     for b, (r, lo, hi) in enumerate(parts):
         buf[r:r + 8, lo:hi] = z[r:r + 8, lo:hi] - col[r:r + 8, :]
         if b >= 1:
-            put(b - 1).start()
-        if b == 3:
+            put(b - 1).start(priority=b % 2)
+        if b == 5:
             nin_copy.start()
             row_copy.start()
     put(len(parts) - 1).start()
@@ -426,7 +426,7 @@
         for size in sizes:
             groups.append((at, at + size))
             at += size
-        head = (0, 2 * LANES, 4 * LANES, T)
+        head = (0, 3 * LANES, 5 * LANES, T)
         cfg = (n, T, block, S, S2, n0, float(width * tp_size), head, tuple(groups))
         vmem = pl.BlockSpec(memory_space=pltpu.VMEM)
         hbm = pl.BlockSpec(memory_space=pl.ANY)

time: 189 us -> 189 us (level)
  no operation moved by 1% of the time
where the time goes in v6:
time: 189 us
  Pallas kernels  189 us (100%)
    pallas_call x1, Pallas kernels, per_device(): pl.pallas_call(functools.partial(logits_kernel, cfg), out_shape=(pltpu.VM...  185 us

profile of v6, /device:TPU:0, one launch (start us, length us, event | category | flops | bytes accessed | tf_op | source)
XLA Modules:
  0.0 189.2 jit_solution(6915723980216498817)
XLA Ops:
  0.6 185.3 %shard_map.94 = (f32[64,31360]{1,0:T(8,128)S(1)}, f32[8,128]{1,0:T(8,128)S(1)}, bf16[64,512]{1,0:T(8,128)(2,1)S(1)}) custom-call(bf16[64,512]{1,0:T(8,128)(2,1)} %hid_hbm.1, f32[1,512]{1,0:T(1,128)} %bitcast.6, f32[1,512]{1,0:T(1,128)} %bitcast.7, s32[1,64]{1,0:T(1,128)} %bitcast.10, f32[1,512]{1,0:T(1,128)} %bitcast.8, f32[1,512]{1,0:T(1,128)} %bitcast.9, ...), custom_call_target="tpu_custom_call" | custom-call | tf_op jit(solution)/shard_map/pallas_call | solution.py:434
  185.9 3.3 %shard_map.95 = (f32[64,31360]{1,0:T(8,128)}, f32[1,64]{1,0:T(1,128)}, bf16[64,512]{1,0:T(8,128)(2,1)}) custom-call(f32[64,31360]{1,0:T(8,128)S(1)} %get-tuple-element.9.z, f32[8,128]{1,0:T(8,128)S(1)} %get-tuple-element.10.lse, bf16[64,512]{1,0:T(8,128)(2,1)S(1)} %get-tuple-element.11.nin), custom_call_target="tpu_custom_call" | custom-call | tf_op jit(solution)/shard_map/pallas_call | solution.py:490

commit v7 on v6

--- a/solution.py
+++ b/solution.py
@@ -54,8 +54,8 @@
     hds_sem, hdr_sem, hxr_sem, extra, extra_sem,
     xn, out, xrecv, drecv, stg, tbuf, pick, ypick, runmax, runsum,
     ln_send, ln_recv, eln_send, eln_recv, fin_send, fin_recv,
-    tab_sem, dsend_sem, drecv_sem, xsend_sem, xrecv_sem, ysend_sem, yrecv_sem,
-    lns_sem, lnr_sem, els_sem, elr_sem, fis_sem, fir_sem,
+    tab_sem, dsend_sem, drecv_sem, xsend_sem, xrecv_sem, yrecv_sem,
+    lns_sem, lnr_sem, elr_sem, fis_sem, fir_sem,
 ):
     n, T, B, S, S2, n0, full_width, head, groups = cfg
     rows = hid.shape[0]
@@ -125,7 +125,7 @@
 
     pairs = ((hid_hbm, hid), (gain_hbm, gain), (bias_hbm, bias), (tok_hbm, tok),
              (egain_hbm, egain), (ebias_hbm, ebias))
-    loads = [pltpu.make_async_copy(src, dst, in_sem.at[k]) for k, (src, dst) in enumerate(pairs)]
+    loads = [pltpu.make_async_copy(src, dst, in_sem.at[slot]) for slot, (src, dst) in zip((0, 1, 1, 2, 1, 1), pairs)]
     for load in loads:
         load.start()
     for j in range(S):
@@ -138,8 +138,9 @@
 
     for d in (2, 3, 1):
         small_copy(ln_send, ln_recv, lns_sem, lnr_sem, d).start()
-    for load in loads[1:]:
-        load.wait()
+    loads[3].wait()
+    four = fin_recv.at[pl.ds(0, 2)]
+    pltpu.make_async_copy(four, four, in_sem.at[1]).wait()
     eye = (lax.broadcasted_iota(jnp.int32, (rows, rows), 0)
            == lax.broadcasted_iota(jnp.int32, (rows, rows), 1))
     tok_col = jnp.sum(
@@ -309,14 +310,14 @@
     z[:, zcols(n - 1)] = z[:, zcols(n - 1)] + drecv[(2 * n - 1) % S2]
 
     ycopy = pltpu.make_async_remote_copy(
-        src_ref=pick, dst_ref=ypick, send_sem=ysend_sem, recv_sem=yrecv_sem,
+        src_ref=pick, dst_ref=ypick, send_sem=hds_sem, recv_sem=yrecv_sem,
         device_id=peer(4), device_id_type=MESH)
     ycopy.start()
     ycopy.wait()
     tok_rows = pick[...] + ypick[...]
     eln_send[...] = row_sums_tile(tok_rows)
     for d in range(1, 4):
-        small_copy(eln_send, eln_recv, els_sem, elr_sem, d).start()
+        small_copy(eln_send, eln_recv, lns_sem, elr_sem, d).start()
     for g in range(n0, len(groups)):
         x_copy(g).start()
 
@@ -359,7 +360,7 @@
         small_copy(fin_send, fin_recv, fis_sem, fir_sem, d).start()
 
     totals = eln_send[...]
-    wait_small(eln_recv, els_sem, elr_sem)
+    wait_small(eln_recv, lns_sem, elr_sem)
     for d in range(3):
         totals = totals + eln_recv[d]
     nin[...] = norm_rows(pick[...] + ypick[...], totals, egain[...], ebias[...], full_width)
@@ -447,7 +448,7 @@
                 pltpu.VMEM((1, rows), jnp.int32),
                 pltpu.VMEM((1, width), F32),
                 pltpu.VMEM((1, width), F32),
-                dma((6,)),
+                dma((3,)),
                 dma,
                 dma((len(head) - 1,)),
                 dma,
@@ -480,8 +481,6 @@
                 dma,
                 dma,
                 dma,
-                dma,
-                dma,
             ],
             compiler_params=pltpu.CompilerParams(
                 collective_id=0, has_side_effects=True, vmem_limit_bytes=52 * 2**20),

time: 189 us -> 189 us (level)
  no operation moved by 1% of the time
where the time goes in v7:
time: 189 us
  Pallas kernels  189 us (100%)
    pallas_call x1, Pallas kernels, per_device(): pl.pallas_call(functools.partial(logits_kernel, cfg), out_shape=(pltpu.VM...  185 us

profile of v7, /device:TPU:0, one launch (start us, length us, event | category | flops | bytes accessed | tf_op | source)
XLA Modules:
  0.0 189.1 jit_solution(4949813317743899701)
XLA Ops:
  0.6 185.2 %shard_map.94 = (f32[64,31360]{1,0:T(8,128)S(1)}, f32[8,128]{1,0:T(8,128)S(1)}, bf16[64,512]{1,0:T(8,128)(2,1)S(1)}) custom-call(bf16[64,512]{1,0:T(8,128)(2,1)} %hid_hbm.1, f32[1,512]{1,0:T(1,128)} %bitcast.6, f32[1,512]{1,0:T(1,128)} %bitcast.7, s32[1,64]{1,0:T(1,128)} %bitcast.10, f32[1,512]{1,0:T(1,128)} %bitcast.8, f32[1,512]{1,0:T(1,128)} %bitcast.9, ...), custom_call_target="tpu_custom_call" | custom-call | tf_op jit(solution)/shard_map/pallas_call | solution.py:435
  185.9 3.3 %shard_map.95 = (f32[64,31360]{1,0:T(8,128)}, f32[1,64]{1,0:T(1,128)}, bf16[64,512]{1,0:T(8,128)(2,1)}) custom-call(f32[64,31360]{1,0:T(8,128)S(1)} %get-tuple-element.9.z, f32[8,128]{1,0:T(8,128)S(1)} %get-tuple-element.10.lse, bf16[64,512]{1,0:T(8,128)(2,1)S(1)} %get-tuple-element.11.nin), custom_call_target="tpu_custom_call" | custom-call | tf_op jit(solution)/shard_map/pallas_call | solution.py:489

commit v8 on v7

--- a/solution.py
+++ b/solution.py
@@ -55,7 +55,7 @@
     xn, out, xrecv, drecv, stg, tbuf, pick, ypick, runmax, runsum,
     ln_send, ln_recv, eln_send, eln_recv, fin_send, fin_recv,
     tab_sem, dsend_sem, drecv_sem, xsend_sem, xrecv_sem, yrecv_sem,
-    lns_sem, lnr_sem, elr_sem, fis_sem, fir_sem,
+    lns_sem, lnr_sem, elr_sem, fir_sem,
 ):
     n, T, B, S, S2, n0, full_width, head, groups = cfg
     rows = hid.shape[0]
@@ -357,7 +357,7 @@
     exp_sum = jnp.sum(runsum[...] * jnp.exp(runmax[...] - top), axis=1, keepdims=True)
     fin_send[...] = two_rows(col_to_row(top), col_to_row(exp_sum))
     for d in (6, 7, 5, 4, 2, 3, 1):
-        small_copy(fin_send, fin_recv, fis_sem, fir_sem, d).start()
+        small_copy(fin_send, fin_recv, hds_sem, fir_sem, d).start()
 
     totals = eln_send[...]
     wait_small(eln_recv, lns_sem, elr_sem)
@@ -374,7 +374,7 @@
         d2d_copy(j).wait_send()
 
     tiles = [fin_send[...]]
-    wait_small(fin_recv, fis_sem, fir_sem)
+    wait_small(fin_recv, hds_sem, fir_sem)
     for d in range(7):
         tiles.append(fin_recv[d])
     best = tiles[0][0:1, :]
@@ -480,7 +480,6 @@
                 dma,
                 dma,
                 dma,
-                dma,
             ],
             compiler_params=pltpu.CompilerParams(
                 collective_id=0, has_side_effects=True, vmem_limit_bytes=52 * 2**20),

time: 189 us -> 189 us (level)
  no operation moved by 1% of the time
where the time goes in v8:
time: 189 us
  Pallas kernels  188 us (99%)
    pallas_call x1, Pallas kernels, per_device(): pl.pallas_call(functools.partial(logits_kernel, cfg), out_shape=(pltpu.VM...  185 us

profile of v8, /device:TPU:0, one launch (start us, length us, event | category | flops | bytes accessed | tf_op | source)
XLA Modules:
  0.0 189.1 jit_solution(17557751826162752601)
XLA Ops:
  0.6 185.2 %shard_map.94 = (f32[64,31360]{1,0:T(8,128)S(1)}, f32[8,128]{1,0:T(8,128)S(1)}, bf16[64,512]{1,0:T(8,128)(2,1)S(1)}) custom-call(bf16[64,512]{1,0:T(8,128)(2,1)} %hid_hbm.1, f32[1,512]{1,0:T(1,128)} %bitcast.6, f32[1,512]{1,0:T(1,128)} %bitcast.7, s32[1,64]{1,0:T(1,128)} %bitcast.10, f32[1,512]{1,0:T(1,128)} %bitcast.8, f32[1,512]{1,0:T(1,128)} %bitcast.9, ...), custom_call_target="tpu_custom_call" | custom-call | tf_op jit(solution)/shard_map/pallas_call | solution.py:435
  185.8 3.3 %shard_map.95 = (f32[64,31360]{1,0:T(8,128)}, f32[1,64]{1,0:T(1,128)}, bf16[64,512]{1,0:T(8,128)(2,1)}) custom-call(f32[64,31360]{1,0:T(8,128)S(1)} %get-tuple-element.9.z, f32[8,128]{1,0:T(8,128)S(1)} %get-tuple-element.10.lse, bf16[64,512]{1,0:T(8,128)(2,1)S(1)} %get-tuple-element.11.nin), custom_call_target="tpu_custom_call" | custom-call | tf_op jit(solution)/shard_map/pallas_call | solution.py:488
